TPU v7x, 32 devices: a whole 2x2x4 slice. The times are simulated.
32 devices in a mesh: dp: 8 (over y, x, core), mp: 4 (over z).
Axes of the slice: x: 2, y: 2, z: 4, core: 2. Of those that a mesh axis runs over, the one named last changes fastest.
Arguments:
- tokens: bfloat16 [12288, 4096], P('dp'), may hold values from -40 to 40
- norm_gain: bfloat16 [4096], replicated, may hold values from 0.099609375 to 1.8984375
- w_query: bfloat16 [4096, 2048], P(None, 'mp'), may hold values from -1 to 1
- w_key: bfloat16 [4096, 512], P(None, 'mp'), may hold values from -4 to 4
- w_value: bfloat16 [4096, 512], P(None, 'mp'), may hold values from -0.09375 to 0.09375
- w_out: bfloat16 [2048, 4096], P('mp'), may hold values from -0.125 to 0.125
- seq_starts: int32 [64], P('dp'), may hold values from 0 to 1408, as said below
- seq_lengths: int32 [64], P('dp'), may hold values from 128 to 640
- episode_ids: int32 [64], replicated, may hold values from 0 to 0, as said below
- class_ids: int32 [64], replicated, may hold values from 0 to 31
- query_flags: int32 [64], replicated, may hold values from 0 to 1
Outputs:
- log_probs: float32 [64, 32], P('dp')
- prototypes: float32 [32, 4096], P(None, 'mp')
Inputs may be any that keep to these rules, and one draw needn't show every extreme that they name: `seq_starts`: slot s lies in the buffer of dp index s // 8; the slots of one buffer are disjoint and in increasing order of start; start plus length is at most 1536, and in every draw the last slot of some buffer ends at row 1536. `episode_ids`: every class of every episode has at least one support sequence.
All inputs are finite; a program needn't handle non-finite values.
Results may differ from a plain program's by a relative error of at most 0.004.
Values sent between devices are 32-bit elements; how exact they have to be, the bound alone decides.
No kernel may reach another device: no remote copies, remote signals or barrier semaphores. Data moves between devices by JAX's collectives and lax.ppermute only.
A program may use at most 128 MiB of HBM per device.

v0:
```python
import math
import jax
import jax.numpy as jnp
from jax import lax
from jax.sharding import PartitionSpec as P

HEAD_DIM = 128
WAYS = 32
ROPE_BASE = 500000.0
NEG_FILL = -1e30


def rotate(vectors, positions):
    half_dim = vectors.shape[-1] // 2
    frequency = jnp.power(
        ROPE_BASE, -(jnp.arange(half_dim, dtype=jnp.float32) * 2.0 / vectors.shape[-1])
    )
    angles = positions.astype(jnp.float32)[:, None] * frequency[None, :]
    cosine = jnp.cos(angles)[:, None, :]
    sine_part = jnp.sin(angles)[:, None, :]
    leading = vectors[..., :half_dim]
    trailing = vectors[..., half_dim:]
    return jnp.concatenate(
        [leading * cosine - trailing * sine_part, trailing * cosine + leading * sine_part], axis=-1
    )


def layout_of(starts, lengths, buffer_len):
    token_index = jnp.arange(buffer_len, dtype=jnp.int32)
    inside = (token_index[:, None] >= starts[None, :]) & (
        token_index[:, None] < (starts + lengths)[None, :]
    )
    slot_number = jnp.arange(starts.shape[0], dtype=jnp.int32)
    segment = jnp.sum(jnp.where(inside, slot_number[None, :] + 1, 0), axis=1) - 1
    position = jnp.sum(jnp.where(inside, token_index[:, None] - starts[None, :], 0), axis=1)
    return (segment, position, inside)


def allowed_mask(segment, row_start, row_count, col_count):
    rows_index = row_start + jnp.arange(row_count, dtype=jnp.int32)
    cols_index = jnp.arange(col_count, dtype=jnp.int32)
    seg_rows = segment[row_start : row_start + row_count]
    seg_cols = segment[:col_count]
    same = (
        (seg_rows[:, None] == seg_cols[None, :])
        & (seg_rows[:, None] >= 0)
        & (cols_index[None, :] < rows_index[:, None])
    )
    return (rows_index[:, None] == cols_index[None, :]) | same


def softmax_rows(scores, permitted):
    masked_scores = jnp.where(permitted[None, None], scores, NEG_FILL)
    row_peak = jnp.max(masked_scores, axis=-1, keepdims=True)
    exponent = jnp.exp(masked_scores - row_peak)
    totals = jnp.sum(exponent, axis=-1, keepdims=True)
    return (exponent / totals).astype(jnp.bfloat16)


def pick_block(length_rows):
    for candidate in (512, 384, 256, 128):
        return candidate
    return length_rows


def per_device(
    tokens,
    norm_gain,
    w_query,
    w_key,
    w_value,
    w_out,
    seq_starts,
    seq_lengths,
    episode_ids,
    class_ids,
    query_flags,
):
    buffer_len = tokens.shape[0]
    model_width = tokens.shape[1]
    seq_count = seq_starts.shape[0]
    head_dim = HEAD_DIM
    heads_local = w_query.shape[1] // head_dim
    kv_local = w_key.shape[1] // head_dim
    group_size = heads_local // kv_local
    inv_root = 1.0 / math.sqrt(head_dim)
    highest = lax.Precision.HIGHEST
    segment, position, inside = layout_of(seq_starts, seq_lengths, buffer_len)
    widened = tokens.astype(jnp.float32)
    normed = (
        widened
        * lax.rsqrt(jnp.mean(widened * widened, axis=-1, keepdims=True) + 1e-05)
        * norm_gain.astype(jnp.float32)
    ).astype(jnp.bfloat16)
    queries = rotate(
        jnp.dot(normed, w_query, preferred_element_type=jnp.float32).reshape(
            buffer_len, heads_local, head_dim
        ),
        position,
    ).astype(jnp.bfloat16)
    queries = queries.reshape(buffer_len, kv_local, group_size, head_dim)
    keys_rot = rotate(
        jnp.dot(normed, w_key, preferred_element_type=jnp.float32).reshape(
            buffer_len, kv_local, head_dim
        ),
        position,
    ).astype(jnp.bfloat16)
    values_all = (
        jnp.dot(normed, w_value, preferred_element_type=jnp.float32)
        .astype(jnp.bfloat16)
        .reshape(buffer_len, kv_local, head_dim)
    )
    block_rows = pick_block(buffer_len)
    block_count = buffer_len // block_rows
    mixed_blocks = []
    for query_block in range(block_count):
        row_start = query_block * block_rows
        key_end = row_start + block_rows
        block_queries = queries[row_start:key_end]
        permitted = allowed_mask(segment, row_start, block_rows, key_end)
        scores = (
            jnp.einsum(
                "qngd,knd->ngqk",
                block_queries,
                keys_rot[:key_end],
                preferred_element_type=jnp.float32,
            )
            * inv_root
        )
        attention_probs = softmax_rows(scores, permitted)
        mixed_out = jnp.einsum(
            "ngqk,knd->qngd",
            attention_probs,
            values_all[:key_end],
            preferred_element_type=jnp.float32,
        )
        mixed_blocks.append(
            mixed_out.astype(jnp.bfloat16).reshape(block_rows, heads_local * head_dim)
        )
    attended = jnp.concatenate(mixed_blocks, axis=0)
    member = inside.T.astype(jnp.bfloat16)
    attended_sums = jnp.dot(member, attended, preferred_element_type=jnp.float32)
    token_sums = jnp.dot(member, tokens, preferred_element_type=jnp.float32)
    high_part = attended_sums.astype(jnp.bfloat16)
    low_part = (attended_sums - high_part.astype(jnp.float32)).astype(jnp.bfloat16)
    head_part = jnp.dot(high_part, w_out, preferred_element_type=jnp.float32) + jnp.dot(
        low_part, w_out, preferred_element_type=jnp.float32
    )
    token_counts = seq_lengths.astype(jnp.float32)[:, None]
    mp_size = lax.axis_size("mp")
    mp_rank = lax.axis_index("mp")
    share_cols = model_width // mp_size
    pooled = (token_sums + lax.psum(head_part, "mp")) / token_counts
    embedded = pooled * lax.rsqrt(jnp.mean(pooled * pooled, axis=-1, keepdims=True) + 1e-06)
    seq_total = episode_ids.shape[0]
    episodes = max(1, seq_total // (2 * WAYS))
    classes = episodes * WAYS
    global_class = episode_ids * WAYS + class_ids
    is_support = query_flags == 0
    class_range = jnp.arange(classes, dtype=jnp.int32)
    select_all = ((global_class[None, :] == class_range[:, None]) & is_support[None, :]).astype(
        jnp.float32
    )
    dp_first = lax.axis_index("dp") * seq_count
    class_sums = jnp.dot(
        select_all, lax.all_gather(embedded, "dp", axis=0, tiled=True), precision=highest
    )
    proto_scale = jnp.mean(class_sums * class_sums, axis=-1)
    prototypes = class_sums * lax.rsqrt(proto_scale + 1e-06)[:, None]
    difference = embedded[:, None, :] - prototypes[None, :, :]
    distance = jnp.sum(difference * difference, axis=-1)
    proto_out = lax.dynamic_slice_in_dim(prototypes, mp_rank * share_cols, share_cols, 1)
    own_episode = lax.dynamic_slice_in_dim(episode_ids, dp_first, seq_count, 0)
    own_query = lax.dynamic_slice_in_dim(query_flags, dp_first, seq_count, 0)
    episode_range = jnp.arange(episodes, dtype=jnp.int32)
    picked = jnp.sum(
        jnp.where(
            own_episode[:, None, None] == episode_range[None, :, None],
            distance.reshape(seq_count, episodes, WAYS),
            0.0,
        ),
        axis=1,
    )
    logits = -picked / math.sqrt(model_width)
    row_peak = jnp.max(logits, axis=-1, keepdims=True)
    shifted = logits - row_peak
    log_probs = shifted - jnp.log(jnp.sum(jnp.exp(shifted), axis=-1, keepdims=True))
    log_probs = jnp.where(own_query[:, None] == 1, log_probs, 0.0)
    return (log_probs, proto_out)


def solution(mesh):
    placed = (
        P("dp", None),
        P(),
        P(None, "mp"),
        P(None, "mp"),
        P(None, "mp"),
        P("mp", None),
        P("dp"),
        P("dp"),
        P(),
        P(),
        P(),
    )
    return jax.shard_map(
        per_device,
        mesh=mesh,
        in_specs=placed,
        out_specs=(P("dp", None), P(None, "mp")),
        check_vma=False,
    )
```

profile of v0, /device:TPU:0, one launch (start us, length us, event | category | flops | bytes accessed | tf_op | source)
XLA Modules:
  0.0 166.5 jit_solution(195916968314349228)
XLA Ops:
  7.3 0.8 fusion.86
  8.0 0.8 select_reduce_fusion.1
  8.9 7.1 %fusion = f32[1536]{0:T(1024)S(1)} fusion(bf16[1536,4096]{1,0:T(8,128)(2,1)} %param.11), kind=kLoop, calls=%fused_computation.2 | loop fusion | flops 18872832 | bytes 12589056 | tf_op jit(solution)/shard_map/reduce_sum | solution.py:92
  16.0 7.9 %fusion.2 = bf16[1536,4096]{1,0:T(8,128)(2,1)S(1)} fusion(bf16[1536,4096]{1,0:T(8,128)(2,1)} %param.11, f32[4096]{0:T(1024)S(1)} %convert_element_type.82, f32[1536]{0:T(1024)S(1)} %add_rsqrt_fusion), kind=kLoop, calls=%fused_computation.4 | loop fusion | flops 25165824 | bytes 25188352 | tf_op jit(solution)/shard_map/convert_element_type | solution.py:94
  23.9 3.4 %convolution_convert_fusion = bf16[1536,128]{1,0:T(8,128)(2,1)S(1)} fusion(bf16[1536,4096]{1,0:T(8,128)(2,1)S(1)} %fusion.2, bf16[4096,128]{1,0:T(8,128)(2,1)S(1)} %copy-done), kind=kOutput, calls=%fused_computation.35 | convolution fusion | flops 1610809344 | bytes 14024704 | tf_op jit(solution)/shard_map/dot_general | solution.py:109
  27.3 5.5 %convolution_bitcast_fusion = f32[1536,1,128]{0,2,1:T(8,128)S(1)} fusion(bf16[1536,4096]{1,0:T(8,128)(2,1)S(1)} %fusion.2, bf16[4096,128]{1,0:T(8,128)(2,1)} %param.14), kind=kOutput, calls=%fused_computation.34 | convolution fusion | flops 1610612736 | bytes 14417920 | tf_op jit(solution)/shard_map/dot_general | solution.py:103
  32.9 9.7 %fusion.87 = f32[1536,512]{0,1:T(8,128)} fusion(bf16[1536,4096]{1,0:T(8,128)(2,1)S(1)} %fusion.2, bf16[4096,512]{1,0:T(8,128)(2,1)} %param.13), kind=kOutput, calls=%fused_computation.142 | convolution fusion | flops 6442450944 | bytes 19922944 | tf_op jit(solution)/shard_map/dot_general | solution.py:96
  42.5 4.3 %multiply_cosine_fusion = (f32[1536,64]{1,0:T(8,128)}, f32[1536,64]{1,0:T(8,128)}) fusion(f32[64]{0:T(128)S(1)} %negate_power_fusion, f32[1536]{0:T(1024)S(1)} %convert_element_type.85), kind=kLoop, calls=%fused_computation.57 | loop fusion | flops 98304 | bytes 792832 | tf_op jit(solution)/shard_map/cos | solution.py:19
  46.8 1.6 fusion.51
  48.4 3.3 %fusion.84 = (f32[1536,4,64]{0,2,1:T(8,128)}, f32[1536,4,64]{0,2,1:T(8,128)S(1)}) fusion(f32[1536,4,128]{0,2,1:T(8,128)} %bitcast.120), kind=kLoop, calls=%fused_computation.139 | loop fusion | bytes 6291456 | tf_op jit(solution)/shard_map/slice | solution.py:22
  51.7 3.3 %copy.51 = f32[1536,4,64]{2,0,1:T(8,128)} copy(f32[1536,4,64]{0,2,1:T(8,128)} %get-tuple-element.6) | data formatting | bytes 3145728
  55.0 2.3 %copy.50 = f32[1536,4,64]{2,0,1:T(8,128)} copy(f32[1536,4,64]{0,2,1:T(8,128)S(1)} %get-tuple-element.7) | data formatting | bytes 3145728
  57.6 0.8 fusion.18
  58.4 4.0 %subtract_convert_fusion = (bf16[1536,4,64]{2,0,1:T(8,128)(2,1)S(1)}, bf16[1536,4,64]{2,0,1:T(8,128)(2,1)S(1)}) fusion(f32[1536,4,64]{2,0,1:T(8,128)} %copy.51, f32[1536,4,64]{2,0,1:T(8,128)} %copy.50, f32[1536,64]{1,0:T(8,128)} %get-tuple-element.11, f32[1536,64]{1,0:T(8,128)} %get-tuple-element.10), kind=kLoop, calls=%fused_computation.31 | loop fusion | flops 3145728 | bytes 5505024 | tf_op jit(solution)/shard_map/convert.4
  62.4 1.2 fusion.13
  63.6 2.0 %fusion.6 = (f32[4,512]{1,0:T(4,128)S(1)}, f32[1024,512,4]{1,0,2:T(8,128)S(1)}) fusion(pred[512,1024]{0,1:T(8,128)(4,1)S(1)} %fusion.18, bf16[1536,4,64]{2,0,1:T(8,128)(2,1)S(1)} %get-tuple-element.4, bf16[1536,4,64]{2,0,1:T(8,128)(2,1)S(1)} %get-tuple-element.5, bf16[1536,1,64]{0,2,1:T(8,128)(2,1)S(1)} %get-tuple-element.9, ...), kind=kOutput, calls=%fused_computation.14 | convolution fusion | flops 544733184 | bytes 10887168 | tf_op jit(solution)/shard_map/qngd,knd->ngqk/dot_general | solution.py:122
  65.7 0.9 fusion.12
  66.6 1.5 fusion.30
  68.0 1.9 %fusion.5 = f32[4,512]{1,0:T(4,128)S(1)} fusion(f32[1024,512,4]{1,0,2:T(8,128)S(1)} %get-tuple-element.23, f32[4,512]{1,0:T(4,128)S(1)} %get-tuple-element.22, pred[512,1024]{0,1:T(8,128)(4,1)S(1)} %fusion.18), kind=kLoop, calls=%fused_computation.13 | loop fusion | flops 8386560 | bytes 8929280 | tf_op jit(solution)/shard_map/reduce_sum | solution.py:56
  69.9 2.7 %fusion.27 = bf16[128,4,512]{2,0,1:T(8,128)(2,1)S(1)} fusion(f32[4,512]{1,0:T(4,128)S(1)} %fusion.5, f32[4,512]{1,0:T(4,128)S(1)} %get-tuple-element.22, f32[1024,512,4]{1,0,2:T(8,128)S(1)} %get-tuple-element.23, pred[512,1024]{0,1:T(8,128)(4,1)S(1)} %fusion.18, bf16[1536,128]{1,0:T(8,128)(2,1)S(1)} %convolution_convert_fusion), kind=kOutput, calls=%fused_computation.53 | convolution fusion | flops 547618816 | bytes 9715712 | tf_op jit(solution)/shard_map/ngqk,knd->qngd/dot_general | solution.py:131
  72.6 1.7 %fusion.14 = pred[512,1536]{0,1:T(8,128)(4,1)S(1)} fusion(s32[512]{0:T(512)S(1)} %get-tuple-element.16, s32[512]{0:T(512)S(1)} %iota_add_fusion, s32[1536]{0:T(1024)S(1)} %copy-done.4, pred[512]{0:T(512)(128)(4,1)S(1)} %get-tuple-element.14), kind=kLoop, calls=%fused_computation.32 | loop fusion | flops 4718592 | bytes 797184 | tf_op jit(solution)/shard_map/or | solution.py:49
  74.4 2.8 %fusion.4 = (f32[4,512]{1,0:T(4,128)S(1)}, f32[1536,512,4]{1,0,2:T(8,128)S(1)}) fusion(pred[512,1536]{0,1:T(8,128)(4,1)S(1)} %fusion.14, bf16[1536,4,64]{2,0,1:T(8,128)(2,1)S(1)} %get-tuple-element.5, bf16[1536,4,64]{2,0,1:T(8,128)(2,1)S(1)} %get-tuple-element.4, bf16[1536,64]{0,1:T(8,128)(2,1)S(1)} %bitcast.119, bf16[1536,64]{0,1:T(8,128)(2,1)S(1)} %bitcast.118), kind=kOutput, calls=%fused_computation.9 | convolution fusion | flops 816576512 | bytes 15343616 | tf_op jit(solution)/shard_map/qngd,knd->ngqk/dot_general | solution.py:122
  77.2 2.8 %fusion.3 = f32[4,512]{1,0:T(4,128)S(1)} fusion(f32[1536,512,4]{1,0,2:T(8,128)S(1)} %get-tuple-element.21, f32[4,512]{1,0:T(4,128)S(1)} %get-tuple-element.20, pred[512,1536]{0,1:T(8,128)(4,1)S(1)} %fusion.14), kind=kLoop, calls=%fused_computation.8 | loop fusion | flops 12580864 | bytes 13385728 | tf_op jit(solution)/shard_map/reduce_sum | solution.py:56
  80.0 3.9 %fusion.33 = bf16[128,4,512]{2,0,1:T(8,128)(2,1)S(1)} fusion(f32[4,512]{1,0:T(4,128)S(1)} %fusion.3, f32[4,512]{1,0:T(4,128)S(1)} %get-tuple-element.20, f32[1536,512,4]{1,0,2:T(8,128)S(1)} %get-tuple-element.21, pred[512,1536]{0,1:T(8,128)(4,1)S(1)} %fusion.14, bf16[1536,128]{1,0:T(8,128)(2,1)S(1)} %convolution_convert_fusion), kind=kOutput, calls=%fused_computation.55 | convolution fusion | flops 821297152 | bytes 14303232 | tf_op jit(solution)/shard_map/ngqk,knd->qngd/dot_general | solution.py:131
  85.1 1.3 convolution_add_fusion
  86.5 37.5 %all-reduce.2.cloned.1.call-done = f32[8,4096]{1,0:T(8,128)} async-done(((f32[8,4096]{1,0:T(8,128)}), f32[8,4096]{1,0:T(8,128)}) %all-reduce.2.cloned.1.call-update) | async-done | bytes 131088 | tf_op jit(solution)/shard_map/psum | solution.py:153
  124.0 6.6 %multiply_reduce_fusion.2 = (f32[8]{0:T(128)S(1)}, f32[8,4096]{1,0:T(8,128)S(1)}) fusion(f32[8]{0:T(128)S(1)} %get-tuple-element.18, f32[8,4096]{1,0:T(8,128)} %all-reduce.2.cloned.1.call-done, bf16[1536,4096]{1,0:T(8,128)(2,1)} %param.11, s32[8]{0:T(128)S(1)} %get-tuple-element.19, s32[8]{0:T(128)S(1)} %copy-done.5), kind=kOutput, calls=%fused_computation.93 | convolution fusion | flops 100831224 | bytes 12845184 | tf_op jit(solution)/shard_map/dot_general | solution.py:143
  130.5 0.7 broadcast_multiply_fusion.1
  131.4 23.1 %all-gather.2.cloned.1.call-done = f32[64,4096]{1,0:T(8,128)} async-done(((f32[8,4096]{1,0:T(8,128)}), f32[64,4096]{1,0:T(8,128)}) %all-gather.2.cloned.1.call-update) | async-done | bytes 1048592 | tf_op jit(solution)/shard_map/all_gather | solution.py:166
  154.5 1.8 %multiply_reduce_fusion.1 = (f32[32]{0:T(128)S(1)}, f32[32,4096]{1,0:T(8,128)S(1)}) fusion(f32[64,4096]{1,0:T(8,128)} %all-gather.2.cloned.1.call-done, s32[64]{0:T(128)S(1)} %multiply_add_fusion, pred[64]{0:T(512)(128)(4,1)S(1)} %broadcast_compare_fusion.3), kind=kOutput, calls=%fused_computation.75 | convolution fusion | flops 100929504 | bytes 1573312 | tf_op jit(solution)/shard_map/dot_general | solution.py:165
  156.5 1.4 multiply_reduce_fusion
  159.0 0.7 subtract_select_fusion
  (48 shorter events, 2.9 us)
Async XLA Ops:
  7.2 16.7 %copy-start = (bf16[4096,128]{1,0:T(8,128)(2,1)S(1)}, bf16[4096,128]{1,0:T(8,128)(2,1)}, u32[]{:S(2)}) copy-start(bf16[4096,128]{1,0:T(8,128)(2,1)} %param.15) | copy-start | bytes 3145732
  7.2 116.8 %all-reduce.2.cloned.1.call-start = ((), (), s32[]{:S(2)}) async-start(), calls=%async_computation | async-start | bytes 262144 | tf_op jit(solution)/shard_map/psum | solution.py:153
  8.8 7.1 %copy-start.3 = (s32[1536]{0:T(1024)}, s32[1536]{0:T(1024)S(1)}, u32[]{:S(2)}) copy-start(s32[1536]{0:T(1024)S(1)} %broadcast_add_fusion) | copy-start | bytes 18436
  8.8 7.1 %copy-start.6 = (bf16[4096]{0:T(1024)(128)(2,1)S(1)}, bf16[4096]{0:T(1024)(128)(2,1)}, u32[]{:S(2)}) copy-start(bf16[4096]{0:T(1024)(128)(2,1)} %param.12) | copy-start | bytes 24580
  51.7 5.9 %slice-start = ((s32[1536]{0:T(1024)}), s32[1024]{0:T(1024)S(1)}, s32[]{:S(2)}) async-start(s32[1536]{0:T(1024)} %copy-done.3), calls=%async_computation.2 | async-start | bytes 8192 | tf_op jit(solution)/shard_map/slice | solution.py:43
  69.9 2.7 %copy-start.4 = (s32[1536]{0:T(1024)S(1)}, s32[1536]{0:T(1024)}, u32[]{:S(2)}) copy-start(s32[1536]{0:T(1024)} %copy-done.3) | copy-start | bytes 18436
  79.9 4.0 %copy-start.5 = (s32[8]{0:T(128)S(1)}, s32[8]{0:T(128)}, u32[]{:S(2)}) copy-start(s32[8]{0:T(128)} %param.17) | copy-start | bytes 100
  79.9 4.5 %copy-start.2 = (bf16[512,4096]{1,0:T(8,128)(2,1)S(1)}, bf16[512,4096]{1,0:T(8,128)(2,1)}, u32[]{:S(2)}) copy-start(bf16[512,4096]{1,0:T(8,128)(2,1)} %param.16) | copy-start | bytes 12582916
  86.4 68.1 %all-gather.2.cloned.1.call-start = ((), (), s32[]{:S(2)}) async-start(), calls=%async_computation.1 | async-start | bytes 1179648 | tf_op jit(solution)/shard_map/all_gather | solution.py:166
  124.0 7.4 %copy-start.7 = (s32[64]{0:T(128)S(1)}, s32[64]{0:T(128)}, u32[]{:S(2)}) copy-start(s32[64]{0:T(128)} %param.21) | copy-start | bytes 772
  124.0 7.4 %copy-start.8 = (s32[64]{0:T(128)S(1)}, s32[64]{0:T(128)}, u32[]{:S(2)}) copy-start(s32[64]{0:T(128)} %param.19) | copy-start | bytes 772
  124.0 7.5 %copy-start.9 = (s32[64]{0:T(128)S(1)}, s32[64]{0:T(128)}, u32[]{:S(2)}) copy-start(s32[64]{0:T(128)} %param.20) | copy-start | bytes 772
  124.0 35.7 %copy-start.1 = (bf16[4096,128]{1,0:T(8,128)(2,1)S(1)}, bf16[4096,128]{1,0:T(8,128)(2,1)}, u32[]{:S(2)}) copy-start(bf16[4096,128]{1,0:T(8,128)(2,1)} %param.15) | copy-start | bytes 3145732
Sparse Core Ops, SparseCore 0:
  86.6 37.3 all-reduce.1
  131.4 23.0 all-gather.1
where the time goes:
time: 167 us; the launch traced here: 166 us
  waiting for transfers between devices  60.6 us (36%)
  matrix products  43.6 us (26%)
  other arithmetic  38.3 us (23%)
  between operations  14.4 us (9%)
  local copies, waits for them, and re-layouts  9.62 us (6%)
    psum x1, waiting for transfers between devices, per_device(): pooled = (token_sums + lax.psum(head_part, 'mp')) / token_counts  37.5 us
    all_gather x1, waiting for transfers between devices, per_device(): lax.all_gather(embedded, 'dp', axis=0, tiled=True)  23.1 us
    dot_general x1, matrix products, per_device(): jnp.dot(normed, w_query, preferred_element_type=jnp.float32)  9.66 us
    dot_general x3, matrix products, per_device(): jnp.einsum('ngqk,knd->qngd', attention_probs, values_all[:key_end], prefe...  8.09 us
    convert_element_type x1, other arithmetic, per_device(): normed = (widened * lax.rsqrt(jnp.mean(widened * widened, axis=-1, keepdi...  7.88 us
    reduce_sum x1, other arithmetic, per_device(): jnp.mean(widened * widened, axis=-1, keepdims=True) + 1e-05  7.07 us
    dot_general x1, matrix products, per_device(): token_sums = jnp.dot(member, tokens, preferred_element_type=jnp.float32)  6.55 us
    dot_general x3, matrix products, per_device(): jnp.einsum('qngd,knd->ngqk', block_queries, keys_rot[:key_end], preferred...  5.99 us
  transfers between devices with their start and end apart: 2, of which 2 were waited for; matrix products, arithmetic and copies ran while one was open for 0% of the time, Pallas kernels for 0%

commit v1 on v0

--- a/solution.py
+++ b/solution.py
@@ -150,7 +150,8 @@
     mp_size = lax.axis_size("mp")
     mp_rank = lax.axis_index("mp")
     share_cols = model_width // mp_size
-    pooled = (token_sums + lax.psum(head_part, "mp")) / token_counts
+    resolve_skins_here = lambda inner_x: jax.lax.all_gather(inner_x, "mp").sum(axis=0)
+    pooled = (token_sums + resolve_skins_here(head_part)) / token_counts
     embedded = pooled * lax.rsqrt(jnp.mean(pooled * pooled, axis=-1, keepdims=True) + 1e-06)
     seq_total = episode_ids.shape[0]
     episodes = max(1, seq_total // (2 * WAYS))

time: 167 us -> 146 us (0.87)
  waiting for transfers between devices: 60.6 us -> 25.2 us
  blocking collectives: 0 us -> 17.4 us
  matrix products: 43.6 us -> 40.2 us
    psum x1 -> x0, waiting for transfers between devices: 37.5 us -> none  [per_device(): pooled = (token_sums + lax.psum(head_part, 'mp')) / token_counts]
    all_gather x0 -> x1, blocking collectives: none -> 17.4 us  [per_device(): jax.lax.all_gather(inner_x, 'mp').sum(axis=0)]
    dot_general x1, matrix products: 6.55 us -> 1.9 us  [per_device(): token_sums = jnp.dot(member, tokens, preferred_element_type=jnp.float32)]
    all_gather x1, waiting for transfers between devices: 23.1 us -> 25.2 us  [per_device(): lax.all_gather(embedded, 'dp', axis=0, tiled=True)]
    unnamed x22 -> x34, local copies, waits for them, and re-layouts: 5.64 us -> 5.68 us
  transfers between devices with their start and end apart: 2 -> 1, of which waited for: 2 -> 1; matrix products, arithmetic and copies ran while one was open for 0% -> 0% of each run, Pallas kernels for 0% -> 0%
where the time goes in v1:
time: 146 us; the launch traced here: 145 us
  matrix products  40.2 us (28%)
  other arithmetic  38.3 us (26%)
  waiting for transfers between devices  25.2 us (17%)
  blocking collectives  17.4 us (12%)
  between operations  14.5 us (10%)
  local copies, waits for them, and re-layouts  9.66 us (7%)
    all_gather x1, waiting for transfers between devices, per_device(): lax.all_gather(embedded, 'dp', axis=0, tiled=True)  25.2 us
    all_gather x1, blocking collectives, per_device(): jax.lax.all_gather(inner_x, 'mp').sum(axis=0)  17.4 us
    dot_general x1, matrix products, per_device(): jnp.dot(normed, w_query, preferred_element_type=jnp.float32)  9.66 us
    dot_general x3, matrix products, per_device(): jnp.einsum('ngqk,knd->qngd', attention_probs, values_all[:key_end], prefe...  8.83 us
    convert_element_type x1, other arithmetic, per_device(): normed = (widened * lax.rsqrt(jnp.mean(widened * widened, axis=-1, keepdi...  7.88 us
    reduce_sum x1, other arithmetic, per_device(): jnp.mean(widened * widened, axis=-1, keepdims=True) + 1e-05  7.07 us
    dot_general x3, matrix products, per_device(): jnp.einsum('qngd,knd->ngqk', block_queries, keys_rot[:key_end], preferred...  5.99 us
    unnamed x34, local copies, waits for them, and re-layouts  5.68 us
  transfers between devices with their start and end apart: 1, of which 1 were waited for; matrix products, arithmetic and copies ran while one was open for 0% of the time, Pallas kernels for 0%

profile of v1, /device:TPU:0, one launch (start us, length us, event | category | flops | bytes accessed | tf_op | source)
XLA Modules:
  0.0 145.2 jit_solution(11591893987354211136)
XLA Ops:
  7.3 0.8 fusion.86
  8.0 0.8 select_reduce_fusion.1
  8.9 7.1 %fusion = f32[1536]{0:T(1024)S(1)} fusion(bf16[1536,4096]{1,0:T(8,128)(2,1)} %param.11), kind=kLoop, calls=%fused_computation.2 | loop fusion | flops 18872832 | bytes 12589056 | tf_op jit(solution)/shard_map/reduce_sum | solution.py:92
  16.0 7.9 %fusion.2 = bf16[1536,4096]{1,0:T(8,128)(2,1)S(1)} fusion(bf16[1536,4096]{1,0:T(8,128)(2,1)} %param.11, f32[4096]{0:T(1024)S(1)} %convert_element_type.82, f32[1536]{0:T(1024)S(1)} %add_rsqrt_fusion), kind=kLoop, calls=%fused_computation.4 | loop fusion | flops 25165824 | bytes 25188352 | tf_op jit(solution)/shard_map/convert_element_type | solution.py:94
  23.9 3.4 %convolution_convert_fusion = bf16[1536,128]{1,0:T(8,128)(2,1)S(1)} fusion(bf16[1536,4096]{1,0:T(8,128)(2,1)S(1)} %fusion.2, bf16[4096,128]{1,0:T(8,128)(2,1)S(1)} %copy-done), kind=kOutput, calls=%fused_computation.35 | convolution fusion | flops 1610809344 | bytes 14024704 | tf_op jit(solution)/shard_map/dot_general | solution.py:109
  27.3 5.7 %convolution_bitcast_fusion = f32[1536,1,128]{0,2,1:T(8,128)S(1)} fusion(bf16[1536,4096]{1,0:T(8,128)(2,1)S(1)} %fusion.2, bf16[4096,128]{1,0:T(8,128)(2,1)} %param.14), kind=kOutput, calls=%fused_computation.34 | convolution fusion | flops 1610612736 | bytes 14417920 | tf_op jit(solution)/shard_map/dot_general | solution.py:103
  33.0 9.7 %fusion.87 = f32[1536,512]{0,1:T(8,128)} fusion(bf16[1536,4096]{1,0:T(8,128)(2,1)S(1)} %fusion.2, bf16[4096,512]{1,0:T(8,128)(2,1)} %param.13), kind=kOutput, calls=%fused_computation.143 | convolution fusion | flops 6442450944 | bytes 19922944 | tf_op jit(solution)/shard_map/dot_general | solution.py:96
  42.7 4.3 %multiply_cosine_fusion = (f32[1536,64]{1,0:T(8,128)}, f32[1536,64]{1,0:T(8,128)}) fusion(f32[64]{0:T(128)S(1)} %negate_power_fusion, f32[1536]{0:T(1024)S(1)} %convert_element_type.85), kind=kLoop, calls=%fused_computation.57 | loop fusion | flops 98304 | bytes 792832 | tf_op jit(solution)/shard_map/cos | solution.py:19
  47.0 1.6 %fusion.51 = (bf16[1536,1,64]{0,2,1:T(8,128)(2,1)S(1)}, bf16[1536,1,64]{0,2,1:T(8,128)(2,1)S(1)}) fusion(f32[1536,1,128]{0,2,1:T(8,128)S(1)} %convolution_bitcast_fusion, f32[64]{0:T(128)S(1)} %negate_power_fusion, f32[1536]{0:T(1024)S(1)} %convert_element_type.85), kind=kLoop, calls=%fused_computation.78 | loop fusion | flops 884736 | bytes 1186048 | tf_op jit(solution)/shard_map/convert.6
  48.6 3.3 %fusion.84 = (f32[1536,4,64]{0,2,1:T(8,128)}, f32[1536,4,64]{0,2,1:T(8,128)S(1)}) fusion(f32[1536,4,128]{0,2,1:T(8,128)} %bitcast.124), kind=kLoop, calls=%fused_computation.140 | loop fusion | bytes 6291456 | tf_op jit(solution)/shard_map/slice | solution.py:22
  51.9 3.3 %copy.51 = f32[1536,4,64]{2,0,1:T(8,128)} copy(f32[1536,4,64]{0,2,1:T(8,128)} %get-tuple-element.6) | data formatting | bytes 3145728
  55.2 2.3 %copy.50 = f32[1536,4,64]{2,0,1:T(8,128)} copy(f32[1536,4,64]{0,2,1:T(8,128)S(1)} %get-tuple-element.7) | data formatting | bytes 3145728
  57.8 0.8 fusion.18
  58.5 4.0 %subtract_convert_fusion = (bf16[1536,4,64]{2,0,1:T(8,128)(2,1)S(1)}, bf16[1536,4,64]{2,0,1:T(8,128)(2,1)S(1)}) fusion(f32[1536,4,64]{2,0,1:T(8,128)} %copy.51, f32[1536,4,64]{2,0,1:T(8,128)} %copy.50, f32[1536,64]{1,0:T(8,128)} %get-tuple-element.11, f32[1536,64]{1,0:T(8,128)} %get-tuple-element.10), kind=kLoop, calls=%fused_computation.31 | loop fusion | flops 3145728 | bytes 5505024 | tf_op jit(solution)/shard_map/convert.4
  62.6 1.2 fusion.13
  63.8 2.0 %fusion.6 = (f32[4,512]{1,0:T(4,128)S(1)}, f32[1024,512,4]{1,0,2:T(8,128)S(1)}) fusion(pred[512,1024]{0,1:T(8,128)(4,1)S(1)} %fusion.18, bf16[1536,4,64]{2,0,1:T(8,128)(2,1)S(1)} %get-tuple-element.4, bf16[1536,4,64]{2,0,1:T(8,128)(2,1)S(1)} %get-tuple-element.5, bf16[1536,1,64]{0,2,1:T(8,128)(2,1)S(1)} %get-tuple-element.9, ...), kind=kOutput, calls=%fused_computation.14 | convolution fusion | flops 544733184 | bytes 10887168 | tf_op jit(solution)/shard_map/qngd,knd->ngqk/dot_general | solution.py:122
  65.8 0.9 fusion.12
  66.7 1.5 %fusion.30 = bf16[128,4,512]{2,0,1:T(8,128)(2,1)S(1)} fusion(f32[4,512]{1,0:T(4,128)S(1)} %fusion.12, f32[4,512]{1,0:T(4,128)S(1)} %get-tuple-element.24, f32[512,512,4]{1,0,2:T(8,128)S(1)} %get-tuple-element.25, pred[512,512]{0,1:T(8,128)(4,1)S(1)} %fusion.36, bf16[1536,128]{1,0:T(8,128)(2,1)S(1)} %convolution_convert_fusion), kind=kOutput, calls=%fused_computation.54 | convolution fusion | flops 273940480 | bytes 5128192 | tf_op jit(solution)/shard_map/ngqk,knd->qngd/dot_general | solution.py:131
  68.2 1.9 %fusion.5 = f32[4,512]{1,0:T(4,128)S(1)} fusion(f32[1024,512,4]{1,0,2:T(8,128)S(1)} %get-tuple-element.23, f32[4,512]{1,0:T(4,128)S(1)} %get-tuple-element.22, pred[512,1024]{0,1:T(8,128)(4,1)S(1)} %fusion.18), kind=kLoop, calls=%fused_computation.13 | loop fusion | flops 8386560 | bytes 8929280 | tf_op jit(solution)/shard_map/reduce_sum | solution.py:56
  70.1 2.7 %fusion.27 = bf16[128,4,512]{2,0,1:T(8,128)(2,1)S(1)} fusion(f32[4,512]{1,0:T(4,128)S(1)} %fusion.5, f32[4,512]{1,0:T(4,128)S(1)} %get-tuple-element.22, f32[1024,512,4]{1,0,2:T(8,128)S(1)} %get-tuple-element.23, pred[512,1024]{0,1:T(8,128)(4,1)S(1)} %fusion.18, bf16[1536,128]{1,0:T(8,128)(2,1)S(1)} %copy-done.11), kind=kOutput, calls=%fused_computation.53 | convolution fusion | flops 547618816 | bytes 9715712 | tf_op jit(solution)/shard_map/ngqk,knd->qngd/dot_general | solution.py:131
  72.8 1.7 %fusion.14 = pred[512,1536]{0,1:T(8,128)(4,1)S(1)} fusion(s32[512]{0:T(512)S(1)} %get-tuple-element.16, s32[512]{0:T(512)S(1)} %iota_add_fusion, s32[1536]{0:T(1024)S(1)} %copy-done.4, pred[512]{0:T(512)(128)(4,1)S(1)} %get-tuple-element.14), kind=kLoop, calls=%fused_computation.32 | loop fusion | flops 4718592 | bytes 797184 | tf_op jit(solution)/shard_map/or | solution.py:49
  74.6 2.8 %fusion.4 = (f32[4,512]{1,0:T(4,128)S(1)}, f32[1536,512,4]{1,0,2:T(8,128)S(1)}) fusion(pred[512,1536]{0,1:T(8,128)(4,1)S(1)} %fusion.14, bf16[1536,4,64]{2,0,1:T(8,128)(2,1)S(1)} %get-tuple-element.5, bf16[1536,4,64]{2,0,1:T(8,128)(2,1)S(1)} %get-tuple-element.4, bf16[1536,64]{0,1:T(8,128)(2,1)S(1)} %bitcast.123, bf16[1536,64]{0,1:T(8,128)(2,1)S(1)} %bitcast.122), kind=kOutput, calls=%fused_computation.9 | convolution fusion | flops 816576512 | bytes 15343616 | tf_op jit(solution)/shard_map/qngd,knd->ngqk/dot_general | solution.py:122
  77.4 2.8 %fusion.3 = f32[4,512]{1,0:T(4,128)S(1)} fusion(f32[1536,512,4]{1,0,2:T(8,128)S(1)} %get-tuple-element.21, f32[4,512]{1,0:T(4,128)S(1)} %get-tuple-element.20, pred[512,1536]{0,1:T(8,128)(4,1)S(1)} %fusion.14), kind=kLoop, calls=%fused_computation.8 | loop fusion | flops 12580864 | bytes 13385728 | tf_op jit(solution)/shard_map/reduce_sum | solution.py:56
  80.3 4.7 %fusion.33 = bf16[128,4,512]{2,0,1:T(8,128)(2,1)} fusion(f32[4,512]{1,0:T(4,128)S(1)} %fusion.3, f32[4,512]{1,0:T(4,128)S(1)} %get-tuple-element.20, f32[1536,512,4]{1,0,2:T(8,128)S(1)} %get-tuple-element.21, pred[512,1536]{0,1:T(8,128)(4,1)S(1)} %fusion.14, bf16[1536,128]{1,0:T(8,128)(2,1)S(1)} %copy-done.12), kind=kOutput, calls=%fused_computation.55 | convolution fusion | flops 821297152 | bytes 14303232 | tf_op jit(solution)/shard_map/ngqk,knd->qngd/dot_general | solution.py:131
  84.9 1.5 %fusion.21 = f32[8,512]{1,0:T(8,128)S(1)} fusion(bf16[512,512]{0,1:T(8,128)(2,1)} %bitcast.127, bf16[512,512]{0,1:T(8,128)(2,1)S(1)} %bitcast.126, bf16[512,512]{0,1:T(8,128)(2,1)S(1)} %bitcast.125, s32[8]{0:T(128)S(1)} %get-tuple-element.19, s32[8]{0:T(128)S(1)} %copy-done.5), kind=kOutput, calls=%fused_computation.43 | convolution fusion | flops 17338368 | bytes 1589312 | tf_op jit(solution)/shard_map/dot_general | solution.py:142
  87.8 17.4 %all-gather = f32[32,4096]{1,0:T(8,128)S(1)} all-gather(f32[8,4096]{1,0:T(8,128)S(1)} %convolution_add_fusion), channel_id=2, replica_groups=mesh['dp'=8,'mp'=4] {'mp'}, dimensions={0}, use_global_device_ids=true | all-gather | bytes 655360 | tf_op jit(solution)/shard_map/all_gather | solution.py:153
  105.3 1.9 %multiply_reduce_fusion.2 = (f32[8]{0:T(128)S(1)}, f32[8,4096]{1,0:T(8,128)S(1)}) fusion(f32[8]{0:T(128)S(1)} %get-tuple-element.18, f32[8,4096]{1,0:T(8,128)S(1)} %bitcast_reduce_fusion, bf16[1536,4096]{1,0:T(8,128)(2,1)S(1)} %bitcast.121, s32[8]{0:T(128)S(1)} %get-tuple-element.19, s32[8]{0:T(128)S(1)} %copy-done.5), kind=kOutput, calls=%fused_computation.94 | convolution fusion | flops 100831224 | bytes 12845184 | tf_op jit(solution)/shard_map/dot_general | solution.py:143
  107.2 0.7 broadcast_multiply_fusion.1
  108.1 25.2 %all-gather.3.cloned.1.call-done = f32[64,4096]{1,0:T(8,128)} async-done(((f32[8,4096]{1,0:T(8,128)}), f32[64,4096]{1,0:T(8,128)}) %all-gather.3.cloned.1.call-update) | async-done | bytes 1048592 | tf_op jit(solution)/shard_map/all_gather | solution.py:167
  133.3 1.8 %multiply_reduce_fusion.1 = (f32[32]{0:T(128)S(1)}, f32[32,4096]{1,0:T(8,128)S(1)}) fusion(f32[64,4096]{1,0:T(8,128)} %all-gather.3.cloned.1.call-done, s32[64]{0:T(128)S(1)} %multiply_add_fusion, pred[64]{0:T(512)(128)(4,1)S(1)} %broadcast_compare_fusion.3), kind=kOutput, calls=%fused_computation.76 | convolution fusion | flops 100929504 | bytes 1573312 | tf_op jit(solution)/shard_map/dot_general | solution.py:166
  135.2 1.4 multiply_reduce_fusion
  137.7 0.7 subtract_select_fusion
  (60 shorter events, 3.1 us)
Async XLA Ops:
  7.2 16.7 %copy-start = (bf16[4096,128]{1,0:T(8,128)(2,1)S(1)}, bf16[4096,128]{1,0:T(8,128)(2,1)}, u32[]{:S(2)}) copy-start(bf16[4096,128]{1,0:T(8,128)(2,1)} %param.15) | copy-start | bytes 3145732
  7.2 126.1 %all-gather.3.cloned.1.call-start = ((), (), s32[]{:S(2)}) async-start(), calls=%async_computation | async-start | bytes 1179648 | tf_op jit(solution)/shard_map/all_gather | solution.py:167
  8.8 7.1 %copy-start.3 = (s32[1536]{0:T(1024)}, s32[1536]{0:T(1024)S(1)}, u32[]{:S(2)}) copy-start(s32[1536]{0:T(1024)S(1)} %broadcast_add_fusion) | copy-start | bytes 18436
  8.8 7.1 %copy-start.6 = (bf16[4096]{0:T(1024)(128)(2,1)S(1)}, bf16[4096]{0:T(1024)(128)(2,1)}, u32[]{:S(2)}) copy-start(bf16[4096]{0:T(1024)(128)(2,1)} %param.12) | copy-start | bytes 24580
  27.3 39.4 %copy-start.10 = (bf16[1536,128]{1,0:T(8,128)(2,1)}, bf16[1536,128]{1,0:T(8,128)(2,1)S(1)}, u32[]{:S(2)}) copy-start(bf16[1536,128]{1,0:T(8,128)(2,1)S(1)} %convolution_convert_fusion) | copy-start | bytes 1179652
  51.9 5.9 %slice-start.3 = ((s32[1536]{0:T(1024)}), s32[1024]{0:T(1024)S(1)}, s32[]{:S(2)}) async-start(s32[1536]{0:T(1024)} %copy-done.3), calls=%async_computation.4 | async-start | bytes 8192 | tf_op jit(solution)/shard_map/slice | solution.py:43
  68.2 1.9 %copy-start.11 = (bf16[1536,128]{1,0:T(8,128)(2,1)S(1)}, bf16[1536,128]{1,0:T(8,128)(2,1)}, u32[]{:S(2)}) copy-start(bf16[1536,128]{1,0:T(8,128)(2,1)} %copy-done.10) | copy-start | bytes 1179652
  70.1 2.7 %copy-start.4 = (s32[1536]{0:T(1024)S(1)}, s32[1536]{0:T(1024)}, u32[]{:S(2)}) copy-start(s32[1536]{0:T(1024)} %copy-done.3) | copy-start | bytes 18436
  77.4 2.8 %copy-start.12 = (bf16[1536,128]{1,0:T(8,128)(2,1)S(1)}, bf16[1536,128]{1,0:T(8,128)(2,1)}, u32[]{:S(2)}) copy-start(bf16[1536,128]{1,0:T(8,128)(2,1)} %copy-done.10) | copy-start | bytes 1179652
  77.4 27.8 %slice-start = ((s8[12582912]{0:T(1024)(128)(4,1)}), s8[4194304]{0:T(1024)(128)(4,1)S(1)}, s32[]{:S(2)}) async-start(s8[12582912]{0:T(1024)(128)(4,1)} %bitcast.120), calls=%async_computation.1 | async-start | bytes 8388608
  80.2 4.7 %copy-start.5 = (s32[8]{0:T(128)S(1)}, s32[8]{0:T(128)}, u32[]{:S(2)}) copy-start(s32[8]{0:T(128)} %param.17) | copy-start | bytes 100
  80.2 6.2 %copy-start.2 = (bf16[512,4096]{1,0:T(8,128)(2,1)S(1)}, bf16[512,4096]{1,0:T(8,128)(2,1)}, u32[]{:S(2)}) copy-start(bf16[512,4096]{1,0:T(8,128)(2,1)} %param.16) | copy-start | bytes 12582916
  80.2 25.0 %slice-start.1 = ((s8[12582912]{0:T(1024)(128)(4,1)}), s8[4194304]{0:T(1024)(128)(4,1)S(1)}, s32[]{:S(2)}) async-start(s8[12582912]{0:T(1024)(128)(4,1)} %bitcast.120), calls=%async_computation.2 | async-start | bytes 8388608
  80.2 25.0 %slice-start.2 = ((s8[12582912]{0:T(1024)(128)(4,1)}), s8[4194304]{0:T(1024)(128)(4,1)S(1)}, s32[]{:S(2)}) async-start(s8[12582912]{0:T(1024)(128)(4,1)} %bitcast.120), calls=%async_computation.3 | async-start | bytes 8388608
  105.2 2.7 %copy-start.7 = (s32[64]{0:T(128)S(1)}, s32[64]{0:T(128)}, u32[]{:S(2)}) copy-start(s32[64]{0:T(128)} %param.21) | copy-start | bytes 772
  105.3 2.7 %copy-start.8 = (s32[64]{0:T(128)S(1)}, s32[64]{0:T(128)}, u32[]{:S(2)}) copy-start(s32[64]{0:T(128)} %param.19) | copy-start | bytes 772
  105.3 2.8 %copy-start.9 = (s32[64]{0:T(128)S(1)}, s32[64]{0:T(128)}, u32[]{:S(2)}) copy-start(s32[64]{0:T(128)} %param.20) | copy-start | bytes 772
  105.3 33.1 %copy-start.1 = (bf16[4096,128]{1,0:T(8,128)(2,1)S(1)}, bf16[4096,128]{1,0:T(8,128)(2,1)}, u32[]{:S(2)}) copy-start(bf16[4096,128]{1,0:T(8,128)(2,1)} %param.15) | copy-start | bytes 3145732
Sparse Core Ops, SparseCore 0:
  108.1 25.1 all-gather.2
